TPU v7x, 32 devices: a whole 2x2x4 slice. The times are simulated.
32 devices in a mesh: groups: 2 (over x), win: 16 (over z, y, core).
Axes of the slice: x: 2, y: 2, z: 4, core: 2. Of those that a mesh axis runs over, the one named last changes fastest.
Arguments:
- latents: bfloat16 [6, 8, 256, 1536], P('groups', None, 'win'), parts along dimension 0, may hold values from -60 to 60
- offsets: int32 [6], P('groups'), parts along dimension 0, may hold values from 0 to 8, as said below
- levels: int32 [6], P('groups'), parts along dimension 0, may hold values from 0 to 31
- mod_table: bfloat16 [32, 6, 1536], replicated, may hold values from -3 to 3
- rel_bias: float32 [6, 64, 64], replicated, may hold values from -3 to 403
- w_qkv: bfloat16 [1536, 2304], P('win'), may hold values from -0.15625 to 0.15625
- w_out: bfloat16 [768, 1536], P('win'), may hold values from -0.21875 to 0.21875
- w_up: bfloat16 [1536, 3072], P('win'), may hold values from -0.15625 to 0.15625
- w_down: bfloat16 [3072, 1536], P('win'), may hold values from -0.109375 to 0.109375
Outputs:
- result: bfloat16 [6, 8, 256, 1536], P('groups', None, 'win'), parts along dimension 0
There are 2 independent parts, one for each index of `groups`. A program takes and returns all parts, laid end to end along the dimension named above; an argument that names none is the same for every part. Nothing has to cross between parts.
Inputs may be any that keep to these rules, and one draw needn't show every extreme that they name: `offsets`: some micro-batch has offset 8 in every draw.
All inputs are finite; a program needn't handle non-finite values.
Results may differ from a plain program's by a relative error of at most 0.007.
Values may be sent and summed in bfloat16 or wider, within the bound.
No kernel may reach another device: no remote copies, remote signals or barrier semaphores. Data moves between devices by JAX's collectives and lax.ppermute only.
A program may use at most 128 MiB of HBM per device.

v0:
```python
import jax
import jax.numpy as jnp
from jax import lax
from jax.sharding import PartitionSpec as P

HEADS = 6
HEAD_DIM = 128
WIN = 8
LEVELS = 32


def passed_along(shard, axis, by):
    length = lax.axis_size(axis)
    return lax.ppermute(shard, axis, [(i, (i + by) % length) for i in range(length)])


def norm_rows(values_in):
    centre = values_in - jnp.mean(values_in, axis=-1, keepdims=True)
    spread = jnp.mean(centre * centre, axis=-1, keepdims=True)
    return centre * lax.rsqrt(spread + 1e-06)


def restore_grid(region, arrived, offsets, columns):
    widened = jnp.concatenate([region, arrived], axis=2)
    return jax.vmap(lambda plane, shift_by: lax.dynamic_slice_in_dim(plane, shift_by, columns, 1))(
        widened, offsets
    )


def local(latents, offsets, levels, mod_table, rel_bias, w_qkv, w_out, w_up, w_down):
    batches, lat_rows, columns, features = latents.shape
    inner = HEADS * HEAD_DIM
    per_dev = columns // WIN
    selector = (levels[:, None] == jnp.arange(LEVELS, dtype=jnp.int32)[None, :]).astype(
        jnp.bfloat16
    )
    modulation = jnp.dot(
        selector, mod_table.reshape(LEVELS, 6 * features), preferred_element_type=jnp.float32
    )
    modulation = modulation.reshape(batches, 6, 1, 1, features)
    stream = latents.astype(jnp.float32)
    normed = (norm_rows(stream) * (1.0 + modulation[:, 0]) + modulation[:, 1]).astype(jnp.bfloat16)
    arrived = passed_along(normed[:, :, columns - WIN :, :], "win", 1)
    widened = jnp.concatenate([arrived, normed], axis=2)
    rolled = jax.vmap(
        lambda plane, shift_by: lax.dynamic_slice_in_dim(plane, WIN - shift_by, columns, 1)
    )(widened, offsets)
    full_qkv = lax.all_gather(w_qkv, "win", axis=0, tiled=True)
    windows = rolled.reshape(batches, lat_rows, per_dev, WIN, features).transpose(0, 2, 1, 3, 4)
    windows = windows.reshape(-1, lat_rows * WIN, features)
    number = windows.shape[0]
    triple = jnp.dot(windows.reshape(-1, features), full_qkv, preferred_element_type=jnp.float32)
    triple = triple.astype(jnp.bfloat16).reshape(number, lat_rows * WIN, 3, HEADS, HEAD_DIM)
    scores = jnp.einsum(
        "wqhe,wkhe->whqk", triple[:, :, 0], triple[:, :, 1], preferred_element_type=jnp.float32
    )
    scores = scores * (1.0 / HEAD_DIM**0.5) + rel_bias[None]
    probs = jax.nn.softmax(scores, axis=-1).astype(jnp.bfloat16)
    attended = jnp.einsum(
        "whqk,wkhe->wqhe", probs, triple[:, :, 2], preferred_element_type=jnp.float32
    ).astype(jnp.bfloat16)
    attended = attended.reshape(batches, per_dev, lat_rows, WIN, inner).transpose(0, 2, 1, 3, 4)
    attended = attended.reshape(batches, lat_rows, columns, inner)
    full_out = lax.all_gather(w_out, "win", axis=0, tiled=True)
    returned = passed_along(attended[:, :, :WIN, :], "win", -1)
    restored = restore_grid(attended, returned, offsets, columns)
    projected = jnp.dot(restored.reshape(-1, inner), full_out, preferred_element_type=jnp.float32)
    projected = projected.reshape(batches, lat_rows, columns, features)
    middle = (stream + modulation[:, 2] * projected).astype(jnp.bfloat16)
    second = (
        norm_rows(middle.astype(jnp.float32)) * (1.0 + modulation[:, 3]) + modulation[:, 4]
    ).astype(jnp.bfloat16)
    full_up = lax.all_gather(w_up, "win", axis=0, tiled=True)
    hidden = jnp.dot(second.reshape(-1, features), full_up, preferred_element_type=jnp.float32)
    hidden = jax.nn.gelu(hidden, approximate=False).astype(jnp.bfloat16)
    full_down = lax.all_gather(w_down, "win", axis=0, tiled=True)
    lowered = jnp.dot(hidden, full_down, preferred_element_type=jnp.float32).reshape(
        batches, lat_rows, columns, features
    )
    return (middle.astype(jnp.float32) + modulation[:, 5] * lowered).astype(jnp.bfloat16)


def solution(mesh):
    in_specs = (
        P("groups", None, "win", None),
        P("groups"),
        P("groups"),
        P(),
        P(),
        P("win", None),
        P("win", None),
        P("win", None),
        P("win", None),
    )
    out_specs = P("groups", None, "win", None)
    return jax.shard_map(local, mesh=mesh, in_specs=in_specs, out_specs=out_specs, check_vma=False)
```

profile of v0, /device:TPU:0, one launch (start us, length us, event | category | flops | bytes accessed | tf_op | source)
XLA Modules:
  0.0 319.7 jit_solution(2629307609174419920)
XLA Ops:
  6.5 0.0 copy-start
  6.5 0.0 copy-start.1
  6.5 0.0 all-gather.5.cloned.1.call-start
  6.5 0.7 all-gather.5.cloned.1.call-update
  7.3 0.0 all-gather.7.cloned.1.call-start
  7.3 0.7 all-gather.7.cloned.1.call-update
  8.0 0.0 all-gather.11.cloned.1.call-start
  8.1 0.7 all-gather.11.cloned.1.call-update
  8.7 0.0 all-gather.9.cloned.1.call-start
  8.8 0.5 all-gather.9.cloned.1.call-update
  9.3 0.0 copy-done
  9.3 0.9 convolution_bitcast_fusion
  10.2 0.0 copy-done.1
  10.2 0.2 convert_reduce_fusion.1
  10.5 0.4 fusion.22
  10.9 0.0 copy-start.6
  11.0 0.7 slice_bitcast_fusion.1
  11.6 0.7 fusion.25
  12.3 0.9 slice.55
  13.2 0.5 collective-permute-start
  13.7 1.7 copy.24
  15.4 0.0 copy-done.6
  15.4 11.6 %collective-permute-done = bf16[3,8,8,1536]{3,2,1,0:T(8,128)(2,1)S(1)} collective-permute-done((bf16[3,8,8,1536]{3,2,1,0:T(8,128)(2,1)}, bf16[3,8,8,1536]{3,2,1,0:T(8,128)(2,1)S(1)}, u32[]{:S(2)}, u32[]{:S(2)}) %collective-permute-start) | collective-permute-done | bytes 589856 | tf_op jit(solution)/shard_map/ppermute | solution.py:14
  27.0 0.1 pad_maximum_fusion
  27.2 0.5 copy.19
  27.7 1.7 gather_fusion
  29.4 2.7 copy.20
  32.0 48.4 %all-gather.5.cloned.1.call-done = bf16[1536,2304]{1,0:T(8,128)(2,1)} async-done(((bf16[96,2304]{1,0:T(8,128)(2,1)}), bf16[1536,2304]{1,0:T(8,128)(2,1)}) %all-gather.5.cloned.1.call-update) | async-done | bytes 7077904 | tf_op jit(solution)/shard_map/all_gather | solution.py:48
  80.5 6.3 %convolution_convert_fusion = bf16[384,2304]{1,0:T(8,128)(2,1)S(1)} fusion(bf16[384,1536]{1,0:T(8,128)(2,1)} %bitcast.93, bf16[1536,2304]{1,0:T(8,128)(2,1)} %all-gather.5.cloned.1.call-done), kind=kOutput, calls=%fused_computation.22 | convolution fusion | flops 2718793728 | bytes 10027008 | tf_op jit(solution)/shard_map/dot_general | solution.py:52
  86.7 3.1 reshape.85
  89.9 0.0 copy-start.2
  89.9 2.9 fusion.109
  92.8 0.0 copy-done.2
  92.8 0.4 fusion.60
  93.3 0.3 fusion.110
  93.6 2.5 fusion.61
  96.0 1.5 copy.26
  97.5 0.7 reshape.86
  98.2 0.1 copy.27
  98.3 2.2 collective-permute-start.1
  100.6 4.2 %collective-permute-done.1 = bf16[3,8,8,768]{3,1,0,2:T(8,128)(2,1)S(1)} collective-permute-done((bf16[3,8,8,768]{3,1,0,2:T(8,128)(2,1)S(1)}, bf16[3,8,8,768]{3,1,0,2:T(8,128)(2,1)S(1)}, u32[]{:S(2)}, u32[]{:S(2)}) %collective-permute-start.1) | collective-permute-done | bytes 294944 | tf_op jit(solution)/shard_map/ppermute | solution.py:14
  104.8 0.1 pad_maximum_fusion.1
  104.9 0.6 gather_fusion.1
  105.5 18.4 %all-gather.7.cloned.1.call-done = bf16[768,1536]{1,0:T(8,128)(2,1)} async-done(((bf16[48,1536]{1,0:T(8,128)(2,1)}), bf16[768,1536]{1,0:T(8,128)(2,1)}) %all-gather.7.cloned.1.call-update) | async-done | bytes 2359312 | tf_op jit(solution)/shard_map/all_gather | solution.py:64
  123.9 0.0 copy-start.4
  123.9 0.0 copy-start.5
  123.9 2.9 convert_reduce_fusion
  126.8 0.4 fusion.18
  127.2 0.0 copy-done.4
  127.2 0.0 copy-done.5
  127.2 0.7 fusion.21
  127.9 77.9 %all-gather.11.cloned.1.call-done = bf16[3072,1536]{1,0:T(8,128)(2,1)} async-done(((bf16[192,1536]{1,0:T(8,128)(2,1)}), bf16[3072,1536]{1,0:T(8,128)(2,1)}) %all-gather.11.cloned.1.call-update) | async-done | bytes 9437200 | tf_op jit(solution)/shard_map/all_gather | solution.py:76
  205.8 81.5 %all-gather.9.cloned.1.call-done = bf16[1536,3072]{1,0:T(8,128)(2,1)} async-done(((bf16[96,3072]{1,0:T(8,128)(2,1)}), bf16[1536,3072]{1,0:T(8,128)(2,1)}) %all-gather.9.cloned.1.call-update) | async-done | bytes 9437200 | tf_op jit(solution)/shard_map/all_gather | solution.py:73
  287.3 0.0 copy-start.3
  287.3 22.8 %fusion.16 = f32[384,1536]{1,0:T(8,128)} fusion(bf16[3072,1536]{1,0:T(8,128)(2,1)} %all-gather.11.cloned.1.call-done, bf16[384,1536]{1,0:T(8,128)(2,1)S(1)} %bitcast.92, bf16[1536,3072]{1,0:T(8,128)(2,1)} %all-gather.9.cloned.1.call-done), kind=kOutput, calls=%fused_computation.35 | convolution fusion | flops 7324434432 | bytes 22413312 | tf_op jit(solution)/shard_map/dot_general | solution.py:77
  310.1 0.0 copy-done.3
  310.1 3.1 fusion.26
  (6 shorter events, 0.1 us)
Async XLA Ops:
  6.5 2.8 copy-start
  6.5 3.7 %copy-start.1 = (bf16[3,8,16,1536]{3,2,1,0:T(8,128)(2,1)S(1)}, bf16[3,8,16,1536]{3,2,1,0:T(8,128)(2,1)}, u32[]{:S(2)}) copy-start(bf16[3,8,16,1536]{3,2,1,0:T(8,128)(2,1)} %param.9) | copy-start | bytes 3538948
  6.5 73.9 %all-gather.5.cloned.1.call-start = ((), (), s32[]{:S(2)}) async-start(), calls=%async_computation | async-start | bytes 7520256 | tf_op jit(solution)/shard_map/all_gather | solution.py:48
  7.3 116.6 %all-gather.7.cloned.1.call-start = ((), (), s32[]{:S(2)}) async-start(), calls=%async_computation.1 | async-start | bytes 2506752 | tf_op jit(solution)/shard_map/all_gather | solution.py:64
  8.0 197.8 %all-gather.11.cloned.1.call-start = ((), (), s32[]{:S(2)}) async-start(), calls=%async_computation.3 | async-start | bytes 10027008 | tf_op jit(solution)/shard_map/all_gather | solution.py:76
  8.7 278.5 %all-gather.9.cloned.1.call-start = ((), (), s32[]{:S(2)}) async-start(), calls=%async_computation.2 | async-start | bytes 10027008 | tf_op jit(solution)/shard_map/all_gather | solution.py:73
  10.9 4.5 %copy-start.6 = (s32[3]{0:T(128)S(1)}, s32[3]{0:T(128)}, u32[]{:S(2)}) copy-start(s32[3]{0:T(128)} %param.10) | copy-start | bytes 40
  13.2 13.9 %collective-permute-start = (bf16[3,8,8,1536]{3,2,1,0:T(8,128)(2,1)}, bf16[3,8,8,1536]{3,2,1,0:T(8,128)(2,1)S(1)}, u32[]{:S(2)}, u32[]{:S(2)}) collective-permute-start(bf16[3,8,8,1536]{3,2,1,0:T(8,128)(2,1)} %slice.55), channel_id=1, source_target_pairs={{0,1},{1,2},{2,3},{3,4},{4,5},{5,6},{6,7},{7,8},{8,9},{9,10},{10,1... | collective-permute-start | bytes 1769480 | tf_op jit(solution)/shard_map/ppermute | solution.py:14
  89.9 2.9 copy-start.2
  98.3 6.5 %collective-permute-start.1 = (bf16[3,8,8,768]{3,1,0,2:T(8,128)(2,1)S(1)}, bf16[3,8,8,768]{3,1,0,2:T(8,128)(2,1)S(1)}, u32[]{:S(2)}, u32[]{:S(2)}) collective-permute-start(bf16[3,8,8,768]{3,1,0,2:T(8,128)(2,1)S(1)} %slice.59), channel_id=1, source_target_pairs={{0,15},{1,0},{2,1},{3,2},{4,3},{5,4},{6,5},{7,6},{8,7},{9,8},{10,9... | collective-permute-start | bytes 884744 | tf_op jit(solution)/shard_map/ppermute | solution.py:14
  123.9 3.4 %copy-start.4 = (f32[3,1536]{1,0:T(4,128)S(1)}, f32[3,1536]{1,0:T(4,128)}, u32[]{:S(2)}) copy-start(f32[3,1536]{1,0:T(4,128)} %get-tuple-element.9) | copy-start | bytes 55300
  123.9 3.4 %copy-start.5 = (f32[3,1536]{1,0:T(4,128)S(1)}, f32[3,1536]{1,0:T(4,128)}, u32[]{:S(2)}) copy-start(f32[3,1536]{1,0:T(4,128)} %get-tuple-element.10) | copy-start | bytes 55300
  287.3 22.9 %copy-start.3 = (f32[3,1536]{1,0:T(4,128)S(1)}, f32[3,1536]{1,0:T(4,128)}, u32[]{:S(2)}) copy-start(f32[3,1536]{1,0:T(4,128)} %get-tuple-element.8) | copy-start | bytes 55300
Sparse Core Ops, SparseCore 0:
  9.6 70.7 all-gather.4
  82.7 41.0 all-gather.6
  126.1 79.6 all-gather.10
  207.9 79.3 all-gather.8
where the time goes:
time: 320 us
  waiting for transfers between devices  245 us (77%)
  matrix products  35.8 us (11%)
  local copies, waits for them, and re-layouts  16.4 us (5%)
  between operations  13.3 us (4%)
  other arithmetic  6.74 us (2%)
    all_gather x1, waiting for transfers between devices, local(): full_up = lax.all_gather(w_up, 'win', axis=0, tiled=True)  81.5 us
    all_gather x1, waiting for transfers between devices, local(): full_down = lax.all_gather(w_down, 'win', axis=0, tiled=True)  77.9 us
    all_gather x1, waiting for transfers between devices, local(): full_qkv = lax.all_gather(w_qkv, 'win', axis=0, tiled=True)  48.4 us
    dot_general x1, matrix products, local(): jnp.dot(hidden, full_down, preferred_element_type=jnp.float32)  22.8 us
    all_gather x1, waiting for transfers between devices, local(): full_out = lax.all_gather(w_out, 'win', axis=0, tiled=True)  18.4 us
    ppermute x2, waiting for transfers between devices, passed_along(): lax.ppermute(shard, axis, [(i, (i + by) % length) for i in range(length)])  15.9 us
  transfers between devices with their start and end apart: 6, of which 6 were waited for; matrix products, arithmetic and copies ran while one was open for 10% of the time, Pallas kernels for 0%

commit v1 on v0

--- a/solution.py
+++ b/solution.py
@@ -1,12 +1,33 @@
+import functools
 import jax
 import jax.numpy as jnp
 from jax import lax
 from jax.sharding import PartitionSpec as P
+from jax.lax import axis_index, axis_size, ppermute
 
 HEADS = 6
 HEAD_DIM = 128
 WIN = 8
 LEVELS = 32
+
+
+def direct_leaf(local_values, peer_axis):
+    n_blocks = axis_size(peer_axis)
+    carry = sorted(((jj, (jj + 1) % n_blocks) for jj in range(n_blocks)))
+    reply = local_values
+    xs_all = [reply]
+    i0 = 1
+    while i0 < n_blocks:
+        reply = ppermute(reply, axis_name=peer_axis, perm=carry)
+        xs_all.insert(0, reply)
+        i0 += 1
+    ready = jnp.concatenate(xs_all, 0)
+    finding = axis_index(peer_axis)
+    then = finding + 1
+    return jnp.roll(ready, then * local_values.shape[0], 0)
+
+
+waves_number = functools.partial(direct_leaf, peer_axis="win")
 
 
 def passed_along(shard, axis, by):
@@ -70,7 +91,7 @@
     second = (
         norm_rows(middle.astype(jnp.float32)) * (1.0 + modulation[:, 3]) + modulation[:, 4]
     ).astype(jnp.bfloat16)
-    full_up = lax.all_gather(w_up, "win", axis=0, tiled=True)
+    full_up = waves_number(w_up)
     hidden = jnp.dot(second.reshape(-1, features), full_up, preferred_element_type=jnp.float32)
     hidden = jax.nn.gelu(hidden, approximate=False).astype(jnp.bfloat16)
     full_down = lax.all_gather(w_down, "win", axis=0, tiled=True)

time: 320 us -> 380 us (1.19)
  local copies, waits for them, and re-layouts: 16.4 us -> 56.4 us
  waiting for transfers between devices: 245 us -> 262 us
    ppermute x0 -> x15, waiting for transfers between devices: none -> 244 us  [direct_leaf(): reply = ppermute(reply, axis_name=peer_axis, perm=carry)]
    all_gather x1 -> x0, waiting for transfers between devices: 81.5 us -> none  [local(): full_up = lax.all_gather(w_up, 'win', axis=0, tiled=True)]
    all_gather x1, waiting for transfers between devices: 77.9 us -> 0.02 us  [local(): full_down = lax.all_gather(w_down, 'win', axis=0, tiled=True)]
    all_gather x1, waiting for transfers between devices: 48.4 us -> 0.01 us  [local(): full_qkv = lax.all_gather(w_qkv, 'win', axis=0, tiled=True)]
    unnamed x15 -> x102, local copies, waits for them, and re-layouts: 1.76 us -> 41.8 us
    all_gather x1, waiting for transfers between devices: 18.4 us -> 0.02 us  [local(): full_out = lax.all_gather(w_out, 'win', axis=0, tiled=True)]
  transfers between devices with their start and end apart: 6 -> 20, of which waited for: 6 -> 17; matrix products, arithmetic and copies ran while one was open for 10% -> 18% of each run, Pallas kernels for 0% -> 0%
where the time goes in v1:
time: 380 us; the launch traced here: 379 us
  waiting for transfers between devices  262 us (69%)
  local copies, waits for them, and re-layouts  56.4 us (15%)
  matrix products  36.1 us (10%)
  between operations  13.4 us (4%)
  other arithmetic  10.1 us (3%)
    ppermute x15, waiting for transfers between devices, direct_leaf(): reply = ppermute(reply, axis_name=peer_axis, perm=carry)  244 us
    unnamed x102, local copies, waits for them, and re-layouts  41.8 us
    dot_general x1, matrix products, local(): jnp.dot(hidden, full_down, preferred_element_type=jnp.float32)  24 us
    ppermute x2, waiting for transfers between devices, passed_along(): lax.ppermute(shard, axis, [(i, (i + by) % length) for i in range(length)])  17.1 us
  transfers between devices with their start and end apart: 20, of which 17 were waited for; matrix products, arithmetic and copies ran while one was open for 18% of the time, Pallas kernels for 0%

profile of v1, /device:TPU:0, one launch (start us, length us, event | category | flops | bytes accessed | tf_op | source)
XLA Modules:
  0.0 379.1 jit_solution(14538247487455385234)
XLA Ops:
  7.9 12.8 %collective-permute-done.2 = bf16[96,3072]{1,0:T(8,128)(2,1)S(1)} collective-permute-done((bf16[96,3072]{1,0:T(8,128)(2,1)}, bf16[96,3072]{1,0:T(8,128)(2,1)S(1)}, u32[]{:S(2)}, u32[]{:S(2)}) %collective-permute-start.2) | collective-permute-done | bytes 589856 | tf_op jit(solution)/shard_map/ppermute | solution.py:21
  21.4 24.5 %collective-permute-done.3 = bf16[96,3072]{1,0:T(8,128)(2,1)S(1)} collective-permute-done((bf16[96,3072]{1,0:T(8,128)(2,1)S(1)}, bf16[96,3072]{1,0:T(8,128)(2,1)S(1)}, u32[]{:S(2)}, u32[]{:S(2)}) %collective-permute-start.3) | collective-permute-done | bytes 589856 | tf_op jit(solution)/shard_map/ppermute | solution.py:21
  46.8 20.7 %collective-permute-done.4 = bf16[96,3072]{1,0:T(8,128)(2,1)S(1)} collective-permute-done((bf16[96,3072]{1,0:T(8,128)(2,1)S(1)}, bf16[96,3072]{1,0:T(8,128)(2,1)S(1)}, u32[]{:S(2)}, u32[]{:S(2)}) %collective-permute-start.4) | collective-permute-done | bytes 589856 | tf_op jit(solution)/shard_map/ppermute | solution.py:21
  67.6 24.7 %collective-permute-done.5 = bf16[96,3072]{1,0:T(8,128)(2,1)S(1)} collective-permute-done((bf16[96,3072]{1,0:T(8,128)(2,1)S(1)}, bf16[96,3072]{1,0:T(8,128)(2,1)S(1)}, u32[]{:S(2)}, u32[]{:S(2)}) %collective-permute-start.5) | collective-permute-done | bytes 589856 | tf_op jit(solution)/shard_map/ppermute | solution.py:21
  92.3 12.0 %collective-permute-done.6 = bf16[96,3072]{1,0:T(8,128)(2,1)S(1)} collective-permute-done((bf16[96,3072]{1,0:T(8,128)(2,1)S(1)}, bf16[96,3072]{1,0:T(8,128)(2,1)S(1)}, u32[]{:S(2)}, u32[]{:S(2)}) %collective-permute-start.6) | collective-permute-done | bytes 589856 | tf_op jit(solution)/shard_map/ppermute | solution.py:21
  105.1 15.2 %collective-permute-done.7 = bf16[96,3072]{1,0:T(8,128)(2,1)S(1)} collective-permute-done((bf16[96,3072]{1,0:T(8,128)(2,1)S(1)}, bf16[96,3072]{1,0:T(8,128)(2,1)S(1)}, u32[]{:S(2)}, u32[]{:S(2)}) %collective-permute-start.7) | collective-permute-done | bytes 589856 | tf_op jit(solution)/shard_map/ppermute | solution.py:21
  121.0 20.2 %collective-permute-done.8 = bf16[96,3072]{1,0:T(8,128)(2,1)S(1)} collective-permute-done((bf16[96,3072]{1,0:T(8,128)(2,1)S(1)}, bf16[96,3072]{1,0:T(8,128)(2,1)S(1)}, u32[]{:S(2)}, u32[]{:S(2)}) %collective-permute-start.8) | collective-permute-done | bytes 589856 | tf_op jit(solution)/shard_map/ppermute | solution.py:21
  142.1 12.0 %collective-permute-done.9 = bf16[96,3072]{1,0:T(8,128)(2,1)S(1)} collective-permute-done((bf16[96,3072]{1,0:T(8,128)(2,1)S(1)}, bf16[96,3072]{1,0:T(8,128)(2,1)S(1)}, u32[]{:S(2)}, u32[]{:S(2)}) %collective-permute-start.9) | collective-permute-done | bytes 589856 | tf_op jit(solution)/shard_map/ppermute | solution.py:21
  154.9 12.0 %collective-permute-done.10 = bf16[96,3072]{1,0:T(8,128)(2,1)S(1)} collective-permute-done((bf16[96,3072]{1,0:T(8,128)(2,1)S(1)}, bf16[96,3072]{1,0:T(8,128)(2,1)S(1)}, u32[]{:S(2)}, u32[]{:S(2)}) %collective-permute-start.10) | collective-permute-done | bytes 589856 | tf_op jit(solution)/shard_map/ppermute | solution.py:21
  167.7 12.0 %collective-permute-done.11 = bf16[96,3072]{1,0:T(8,128)(2,1)S(1)} collective-permute-done((bf16[96,3072]{1,0:T(8,128)(2,1)S(1)}, bf16[96,3072]{1,0:T(8,128)(2,1)S(1)}, u32[]{:S(2)}, u32[]{:S(2)}) %collective-permute-start.11) | collective-permute-done | bytes 589856 | tf_op jit(solution)/shard_map/ppermute | solution.py:21
  179.7 1.7 convert_reduce_fusion.1
  181.4 10.4 %collective-permute-done.12 = bf16[96,3072]{1,0:T(8,128)(2,1)} collective-permute-done((bf16[96,3072]{1,0:T(8,128)(2,1)S(1)}, bf16[96,3072]{1,0:T(8,128)(2,1)}, u32[]{:S(2)}, u32[]{:S(2)}) %collective-permute-start.12) | collective-permute-done | bytes 589856 | tf_op jit(solution)/shard_map/ppermute | solution.py:21
  191.8 1.7 fusion.24
  193.6 23.3 %collective-permute-done.13 = bf16[96,3072]{1,0:T(8,128)(2,1)S(1)} collective-permute-done((bf16[96,3072]{1,0:T(8,128)(2,1)}, bf16[96,3072]{1,0:T(8,128)(2,1)S(1)}, u32[]{:S(2)}, u32[]{:S(2)}) %collective-permute-start.13) | collective-permute-done | bytes 589856 | tf_op jit(solution)/shard_map/ppermute | solution.py:21
  216.8 0.9 convolution_bitcast_fusion
  218.4 11.3 %collective-permute-done.14 = bf16[96,3072]{1,0:T(8,128)(2,1)S(1)} collective-permute-done((bf16[96,3072]{1,0:T(8,128)(2,1)S(1)}, bf16[96,3072]{1,0:T(8,128)(2,1)S(1)}, u32[]{:S(2)}, u32[]{:S(2)}) %collective-permute-start.14) | collective-permute-done | bytes 589856 | tf_op jit(solution)/shard_map/ppermute | solution.py:21
  231.3 0.9 slice.55
  232.1 22.6 %collective-permute-done.15 = bf16[96,3072]{1,0:T(8,128)(2,1)} collective-permute-done((bf16[96,3072]{1,0:T(8,128)(2,1)S(1)}, bf16[96,3072]{1,0:T(8,128)(2,1)}, u32[]{:S(2)}, u32[]{:S(2)}) %collective-permute-start.15) | collective-permute-done | bytes 589856 | tf_op jit(solution)/shard_map/ppermute | solution.py:21
  254.7 1.7 copy.24
  256.4 13.7 %collective-permute-done = bf16[3,8,8,1536]{3,2,1,0:T(8,128)(2,1)S(1)} collective-permute-done((bf16[3,8,8,1536]{3,2,1,0:T(8,128)(2,1)}, bf16[3,8,8,1536]{3,2,1,0:T(8,128)(2,1)S(1)}, u32[]{:S(2)}, u32[]{:S(2)}) %collective-permute-start) | collective-permute-done | bytes 589856 | tf_op jit(solution)/shard_map/ppermute | solution.py:35
  270.9 1.7 gather_fusion
  272.5 2.8 copy.20
  275.3 10.7 %collective-permute-done.16 = bf16[96,3072]{1,0:T(8,128)(2,1)} collective-permute-done((bf16[96,3072]{1,0:T(8,128)(2,1)}, bf16[96,3072]{1,0:T(8,128)(2,1)}, u32[]{:S(2)}, u32[]{:S(2)}) %collective-permute-start.16) | collective-permute-done | bytes 589856 | tf_op jit(solution)/shard_map/ppermute | solution.py:21
  286.0 1.9 constant_dynamic-update-slice_fusion.31
  287.9 2.0 constant_dynamic-update-slice_fusion.30
  289.9 0.9 constant_dynamic-update-slice_fusion.29
  290.8 0.9 constant_dynamic-update-slice_fusion.28
  291.7 2.0 constant_dynamic-update-slice_fusion.27
  293.7 0.9 constant_dynamic-update-slice_fusion.26
  294.5 0.9 constant_dynamic-update-slice_fusion.25
  295.4 0.9 constant_dynamic-update-slice_fusion.24
  296.3 0.9 constant_dynamic-update-slice_fusion.23
  297.2 0.9 constant_dynamic-update-slice_fusion.22
  298.0 0.9 constant_dynamic-update-slice_fusion.21
  298.9 0.9 constant_dynamic-update-slice_fusion.20
  299.8 0.9 constant_dynamic-update-slice_fusion.19
  300.6 0.9 constant_dynamic-update-slice_fusion.18
  301.6 0.9 constant_dynamic-update-slice_fusion.17
  302.5 0.9 constant_dynamic-update-slice_fusion.16
  303.4 1.9 constant_dynamic-update-slice_fusion.15
  305.3 1.9 constant_dynamic-update-slice_fusion.14
  307.2 0.9 constant_dynamic-update-slice_fusion.13
  308.1 0.9 constant_dynamic-update-slice_fusion.12
  308.9 2.0 constant_dynamic-update-slice_fusion.11
  310.9 0.9 constant_dynamic-update-slice_fusion.10
  311.8 0.9 constant_dynamic-update-slice_fusion.9
  312.6 0.8 constant_dynamic-update-slice_fusion.8
  313.5 0.9 constant_dynamic-update-slice_fusion.7
  314.4 0.9 constant_dynamic-update-slice_fusion.6
  315.2 0.9 constant_dynamic-update-slice_fusion.5
  316.1 0.9 constant_dynamic-update-slice_fusion.4
  317.0 0.9 constant_dynamic-update-slice_fusion.3
  317.8 0.9 constant_dynamic-update-slice_fusion.2
  318.7 0.9 constant_dynamic-update-slice_fusion.1
  319.6 6.3 %convolution_convert_fusion = bf16[384,2304]{1,0:T(8,128)(2,1)S(1)} fusion(bf16[384,1536]{1,0:T(8,128)(2,1)} %bitcast.83, bf16[1536,2304]{1,0:T(8,128)(2,1)} %all-gather.4.cloned.1.call-done), kind=kOutput, calls=%fused_computation.24 | convolution fusion | flops 2718793728 | bytes 10027008 | tf_op jit(solution)/shard_map/dot_general | solution.py:73
  325.9 3.1 reshape.85
  329.0 2.9 fusion.117
  332.4 0.9 fusion.118
  333.3 1.6 fusion.67
  336.5 0.9 constant_dynamic-update-slice_fusion
  337.3 3.4 collective-permute-done.1
  341.4 2.9 convert_reduce_fusion
  345.5 24.0 %fusion.18 = f32[384,1536]{1,0:T(8,128)} fusion(bf16[3072,1536]{1,0:T(8,128)(2,1)} %all-gather.8.cloned.1.call-done, bf16[384,1536]{1,0:T(8,128)(2,1)S(1)} %bitcast.84, bf16[3072,3072]{1,0:T(8,128)(2,1)} %constant_dynamic-update-slice_fusion, s32[]{:T(128)S(6)} %select_n.22), kind=kOutput, calls=%fused_computation.37 | convolution fusion | flops 7324434432 | bytes 22413316 | tf_op jit(solution)/shard_map/dot_general | solution.py:98
  369.5 3.1 fusion.28
  (114 shorter events, 13.8 us)
Async XLA Ops:
  6.5 210.3 %copy-start = (bf16[32,6,1536]{2,0,1:T(8,128)(2,1)S(1)}, bf16[32,6,1536]{2,0,1:T(8,128)(2,1)}, u32[]{:S(2)}) copy-start(bf16[32,6,1536]{2,0,1:T(8,128)(2,1)} %param.12) | copy-start | bytes 1769476
  6.5 224.0 %copy-start.2 = (bf16[3,8,16,1536]{3,2,1,0:T(8,128)(2,1)S(1)}, bf16[3,8,16,1536]{3,2,1,0:T(8,128)(2,1)}, u32[]{:S(2)}) copy-start(bf16[3,8,16,1536]{3,2,1,0:T(8,128)(2,1)} %param.9) | copy-start | bytes 3538948
  6.5 249.9 %copy-start.34 = (s32[3]{0:T(128)S(1)}, s32[3]{0:T(128)}, u32[]{:S(2)}) copy-start(s32[3]{0:T(128)} %param.10) | copy-start | bytes 40
  6.5 313.0 %all-gather.4.cloned.1.call-start = ((), (), s32[]{:S(2)}) async-start(), calls=%async_computation | async-start | bytes 7520256 | tf_op jit(solution)/shard_map/all_gather | solution.py:69
  7.3 334.1 %all-gather.6.cloned.1.call-start = ((), (), s32[]{:S(2)}) async-start(), calls=%async_computation.1 | async-start | bytes 2506752 | tf_op jit(solution)/shard_map/all_gather | solution.py:85
  7.3 13.3 %collective-permute-start.2 = (bf16[96,3072]{1,0:T(8,128)(2,1)}, bf16[96,3072]{1,0:T(8,128)(2,1)S(1)}, u32[]{:S(2)}, u32[]{:S(2)}) collective-permute-start(bf16[96,3072]{1,0:T(8,128)(2,1)} %param.16), channel_id=1, source_target_pairs={{0,1},{1,2},{2,3},{3,4},{4,5},{5,6},{6,7},{7,8},{8,9},{9,10},{10,1... | collective-permute-start | bytes 1769480 | tf_op jit(solution)/shard_map/ppermute | solution.py:21
  20.6 0.8 copy-start.4
  21.4 24.5 %collective-permute-start.3 = (bf16[96,3072]{1,0:T(8,128)(2,1)S(1)}, bf16[96,3072]{1,0:T(8,128)(2,1)S(1)}, u32[]{:S(2)}, u32[]{:S(2)}) collective-permute-start(bf16[96,3072]{1,0:T(8,128)(2,1)S(1)} %collective-permute-done.2), channel_id=1, source_target_pairs={{0,1},{1,2},{2,3},{3,4},{4,5},{5,6},{6,7},{7,8},{8,9},{9,10},{10,1... | collective-permute-start | bytes 1769480 | tf_op jit(solution)/shard_map/ppermute | solution.py:21
  45.9 0.8 copy-start.6
  46.8 20.7 %collective-permute-start.4 = (bf16[96,3072]{1,0:T(8,128)(2,1)S(1)}, bf16[96,3072]{1,0:T(8,128)(2,1)S(1)}, u32[]{:S(2)}, u32[]{:S(2)}) collective-permute-start(bf16[96,3072]{1,0:T(8,128)(2,1)S(1)} %collective-permute-done.3), channel_id=1, source_target_pairs={{0,1},{1,2},{2,3},{3,4},{4,5},{5,6},{6,7},{7,8},{8,9},{9,10},{10,1... | collective-permute-start | bytes 1769480 | tf_op jit(solution)/shard_map/ppermute | solution.py:21
  67.5 162.3 %copy-start.8 = (bf16[96,3072]{1,0:T(8,128)(2,1)}, bf16[96,3072]{1,0:T(8,128)(2,1)S(1)}, u32[]{:S(2)}) copy-start(bf16[96,3072]{1,0:T(8,128)(2,1)S(1)} %collective-permute-done.4) | copy-start | bytes 1769476
  67.5 24.8 %collective-permute-start.5 = (bf16[96,3072]{1,0:T(8,128)(2,1)S(1)}, bf16[96,3072]{1,0:T(8,128)(2,1)S(1)}, u32[]{:S(2)}, u32[]{:S(2)}) collective-permute-start(bf16[96,3072]{1,0:T(8,128)(2,1)S(1)} %collective-permute-done.4), channel_id=1, source_target_pairs={{0,1},{1,2},{2,3},{3,4},{4,5},{5,6},{6,7},{7,8},{8,9},{9,10},{10,1... | collective-permute-start | bytes 1769480 | tf_op jit(solution)/shard_map/ppermute | solution.py:21
  67.5 278.0 %all-gather.8.cloned.1.call-start = ((), (), s32[]{:S(2)}) async-start(), calls=%async_computation.2 | async-start | bytes 10027008 | tf_op jit(solution)/shard_map/all_gather | solution.py:97
  92.2 137.5 %copy-start.10 = (bf16[96,3072]{1,0:T(8,128)(2,1)}, bf16[96,3072]{1,0:T(8,128)(2,1)S(1)}, u32[]{:S(2)}) copy-start(bf16[96,3072]{1,0:T(8,128)(2,1)S(1)} %collective-permute-done.5) | copy-start | bytes 1769476
  92.2 12.0 %collective-permute-start.6 = (bf16[96,3072]{1,0:T(8,128)(2,1)S(1)}, bf16[96,3072]{1,0:T(8,128)(2,1)S(1)}, u32[]{:S(2)}, u32[]{:S(2)}) collective-permute-start(bf16[96,3072]{1,0:T(8,128)(2,1)S(1)} %collective-permute-done.5), channel_id=1, source_target_pairs={{0,1},{1,2},{2,3},{3,4},{4,5},{5,6},{6,7},{7,8},{8,9},{9,10},{10,1... | collective-permute-start | bytes 1769480 | tf_op jit(solution)/shard_map/ppermute | solution.py:21
  104.3 0.8 copy-start.12
  105.1 15.2 %collective-permute-start.7 = (bf16[96,3072]{1,0:T(8,128)(2,1)S(1)}, bf16[96,3072]{1,0:T(8,128)(2,1)S(1)}, u32[]{:S(2)}, u32[]{:S(2)}) collective-permute-start(bf16[96,3072]{1,0:T(8,128)(2,1)S(1)} %collective-permute-done.6), channel_id=1, source_target_pairs={{0,1},{1,2},{2,3},{3,4},{4,5},{5,6},{6,7},{7,8},{8,9},{9,10},{10,1... | collective-permute-start | bytes 1769480 | tf_op jit(solution)/shard_map/ppermute | solution.py:21
  120.2 0.8 copy-start.14
  121.0 20.2 %collective-permute-start.8 = (bf16[96,3072]{1,0:T(8,128)(2,1)S(1)}, bf16[96,3072]{1,0:T(8,128)(2,1)S(1)}, u32[]{:S(2)}, u32[]{:S(2)}) collective-permute-start(bf16[96,3072]{1,0:T(8,128)(2,1)S(1)} %collective-permute-done.7), channel_id=1, source_target_pairs={{0,1},{1,2},{2,3},{3,4},{4,5},{5,6},{6,7},{7,8},{8,9},{9,10},{10,1... | collective-permute-start | bytes 1769480 | tf_op jit(solution)/shard_map/ppermute | solution.py:21
  141.2 0.8 copy-start.16
  142.1 12.0 %collective-permute-start.9 = (bf16[96,3072]{1,0:T(8,128)(2,1)S(1)}, bf16[96,3072]{1,0:T(8,128)(2,1)S(1)}, u32[]{:S(2)}, u32[]{:S(2)}) collective-permute-start(bf16[96,3072]{1,0:T(8,128)(2,1)S(1)} %collective-permute-done.8), channel_id=1, source_target_pairs={{0,1},{1,2},{2,3},{3,4},{4,5},{5,6},{6,7},{7,8},{8,9},{9,10},{10,1... | collective-permute-start | bytes 1769480 | tf_op jit(solution)/shard_map/ppermute | solution.py:21
  154.1 0.8 copy-start.18
  154.9 12.0 %collective-permute-start.10 = (bf16[96,3072]{1,0:T(8,128)(2,1)S(1)}, bf16[96,3072]{1,0:T(8,128)(2,1)S(1)}, u32[]{:S(2)}, u32[]{:S(2)}) collective-permute-start(bf16[96,3072]{1,0:T(8,128)(2,1)S(1)} %collective-permute-done.9), channel_id=1, source_target_pairs={{0,1},{1,2},{2,3},{3,4},{4,5},{5,6},{6,7},{7,8},{8,9},{9,10},{10,1... | collective-permute-start | bytes 1769480 | tf_op jit(solution)/shard_map/ppermute | solution.py:21
  166.9 0.8 copy-start.20
  167.7 12.0 %collective-permute-start.11 = (bf16[96,3072]{1,0:T(8,128)(2,1)S(1)}, bf16[96,3072]{1,0:T(8,128)(2,1)S(1)}, u32[]{:S(2)}, u32[]{:S(2)}) collective-permute-start(bf16[96,3072]{1,0:T(8,128)(2,1)S(1)} %collective-permute-done.10), channel_id=1, source_target_pairs={{0,1},{1,2},{2,3},{3,4},{4,5},{5,6},{6,7},{7,8},{8,9},{9,10},{10,1... | collective-permute-start | bytes 1769480 | tf_op jit(solution)/shard_map/ppermute | solution.py:21
  179.7 90.5 %copy-start.22 = (bf16[96,3072]{1,0:T(8,128)(2,1)}, bf16[96,3072]{1,0:T(8,128)(2,1)S(1)}, u32[]{:S(2)}) copy-start(bf16[96,3072]{1,0:T(8,128)(2,1)S(1)} %collective-permute-done.11) | copy-start | bytes 1769476
  179.7 12.1 %collective-permute-start.12 = (bf16[96,3072]{1,0:T(8,128)(2,1)S(1)}, bf16[96,3072]{1,0:T(8,128)(2,1)}, u32[]{:S(2)}, u32[]{:S(2)}) collective-permute-start(bf16[96,3072]{1,0:T(8,128)(2,1)S(1)} %collective-permute-done.11), channel_id=1, source_target_pairs={{0,1},{1,2},{2,3},{3,4},{4,5},{5,6},{6,7},{7,8},{8,9},{9,10},{10,1... | collective-permute-start | bytes 1769480 | tf_op jit(solution)/shard_map/ppermute | solution.py:21
  191.8 25.0 %collective-permute-start.13 = (bf16[96,3072]{1,0:T(8,128)(2,1)}, bf16[96,3072]{1,0:T(8,128)(2,1)S(1)}, u32[]{:S(2)}, u32[]{:S(2)}) collective-permute-start(bf16[96,3072]{1,0:T(8,128)(2,1)} %collective-permute-done.12), channel_id=1, source_target_pairs={{0,1},{1,2},{2,3},{3,4},{4,5},{5,6},{6,7},{7,8},{8,9},{9,10},{10,1... | collective-permute-start | bytes 1769480 | tf_op jit(solution)/shard_map/ppermute | solution.py:21
  216.8 13.0 %copy-start.24 = (bf16[96,3072]{1,0:T(8,128)(2,1)}, bf16[96,3072]{1,0:T(8,128)(2,1)S(1)}, u32[]{:S(2)}) copy-start(bf16[96,3072]{1,0:T(8,128)(2,1)S(1)} %collective-permute-done.13) | copy-start | bytes 1769476
  216.8 12.9 %collective-permute-start.14 = (bf16[96,3072]{1,0:T(8,128)(2,1)S(1)}, bf16[96,3072]{1,0:T(8,128)(2,1)S(1)}, u32[]{:S(2)}, u32[]{:S(2)}) collective-permute-start(bf16[96,3072]{1,0:T(8,128)(2,1)S(1)} %collective-permute-done.13), channel_id=1, source_target_pairs={{0,1},{1,2},{2,3},{3,4},{4,5},{5,6},{6,7},{7,8},{8,9},{9,10},{10,1... | collective-permute-start | bytes 1769480 | tf_op jit(solution)/shard_map/ppermute | solution.py:21
  229.8 0.8 copy-start.27
  229.8 24.9 %collective-permute-start.15 = (bf16[96,3072]{1,0:T(8,128)(2,1)S(1)}, bf16[96,3072]{1,0:T(8,128)(2,1)}, u32[]{:S(2)}, u32[]{:S(2)}) collective-permute-start(bf16[96,3072]{1,0:T(8,128)(2,1)S(1)} %collective-permute-done.14), channel_id=1, source_target_pairs={{0,1},{1,2},{2,3},{3,4},{4,5},{5,6},{6,7},{7,8},{8,9},{9,10},{10,1... | collective-permute-start | bytes 1769480 | tf_op jit(solution)/shard_map/ppermute | solution.py:21
  232.1 38.0 %collective-permute-start = (bf16[3,8,8,1536]{3,2,1,0:T(8,128)(2,1)}, bf16[3,8,8,1536]{3,2,1,0:T(8,128)(2,1)S(1)}, u32[]{:S(2)}, u32[]{:S(2)}) collective-permute-start(bf16[3,8,8,1536]{3,2,1,0:T(8,128)(2,1)} %slice.55), channel_id=1, source_target_pairs={{0,1},{1,2},{2,3},{3,4},{4,5},{5,6},{6,7},{7,8},{8,9},{9,10},{10,1... | collective-permute-start | bytes 1769480 | tf_op jit(solution)/shard_map/ppermute | solution.py:35
  254.7 31.3 %collective-permute-start.16 = (bf16[96,3072]{1,0:T(8,128)(2,1)}, bf16[96,3072]{1,0:T(8,128)(2,1)}, u32[]{:S(2)}, u32[]{:S(2)}) collective-permute-start(bf16[96,3072]{1,0:T(8,128)(2,1)} %collective-permute-done.15), channel_id=1, source_target_pairs={{0,1},{1,2},{2,3},{3,4},{4,5},{5,6},{6,7},{7,8},{8,9},{9,10},{10,1... | collective-permute-start | bytes 1769480 | tf_op jit(solution)/shard_map/ppermute | solution.py:21
  270.8 19.9 %copy-start.25 = (bf16[96,3072]{1,0:T(8,128)(2,1)S(1)}, bf16[96,3072]{1,0:T(8,128)(2,1)}, u32[]{:S(2)}) copy-start(bf16[96,3072]{1,0:T(8,128)(2,1)} %copy-done.24) | copy-start | bytes 1769476
  272.5 17.4 %copy-start.28 = (bf16[96,3072]{1,0:T(8,128)(2,1)S(1)}, bf16[96,3072]{1,0:T(8,128)(2,1)}, u32[]{:S(2)}) copy-start(bf16[96,3072]{1,0:T(8,128)(2,1)} %copy-done.27) | copy-start | bytes 1769476
  272.5 21.1 %copy-start.23 = (bf16[96,3072]{1,0:T(8,128)(2,1)S(1)}, bf16[96,3072]{1,0:T(8,128)(2,1)}, u32[]{:S(2)}) copy-start(bf16[96,3072]{1,0:T(8,128)(2,1)} %copy-done.22) | copy-start | bytes 1769476
  272.5 22.0 %copy-start.21 = (bf16[96,3072]{1,0:T(8,128)(2,1)S(1)}, bf16[96,3072]{1,0:T(8,128)(2,1)}, u32[]{:S(2)}) copy-start(bf16[96,3072]{1,0:T(8,128)(2,1)} %copy-done.20) | copy-start | bytes 1769476
  275.3 20.1 %copy-start.19 = (bf16[96,3072]{1,0:T(8,128)(2,1)S(1)}, bf16[96,3072]{1,0:T(8,128)(2,1)}, u32[]{:S(2)}) copy-start(bf16[96,3072]{1,0:T(8,128)(2,1)} %copy-done.18) | copy-start | bytes 1769476
  275.3 21.0 %copy-start.17 = (bf16[96,3072]{1,0:T(8,128)(2,1)S(1)}, bf16[96,3072]{1,0:T(8,128)(2,1)}, u32[]{:S(2)}) copy-start(bf16[96,3072]{1,0:T(8,128)(2,1)} %copy-done.16) | copy-start | bytes 1769476
  287.9 9.2 %copy-start.15 = (bf16[96,3072]{1,0:T(8,128)(2,1)S(1)}, bf16[96,3072]{1,0:T(8,128)(2,1)}, u32[]{:S(2)}) copy-start(bf16[96,3072]{1,0:T(8,128)(2,1)} %copy-done.14) | copy-start | bytes 1769476
  289.9 8.1 %copy-start.13 = (bf16[96,3072]{1,0:T(8,128)(2,1)S(1)}, bf16[96,3072]{1,0:T(8,128)(2,1)}, u32[]{:S(2)}) copy-start(bf16[96,3072]{1,0:T(8,128)(2,1)} %copy-done.12) | copy-start | bytes 1769476
  290.8 8.1 %copy-start.11 = (bf16[96,3072]{1,0:T(8,128)(2,1)S(1)}, bf16[96,3072]{1,0:T(8,128)(2,1)}, u32[]{:S(2)}) copy-start(bf16[96,3072]{1,0:T(8,128)(2,1)} %copy-done.10) | copy-start | bytes 1769476
  291.7 8.1 %copy-start.9 = (bf16[96,3072]{1,0:T(8,128)(2,1)S(1)}, bf16[96,3072]{1,0:T(8,128)(2,1)}, u32[]{:S(2)}) copy-start(bf16[96,3072]{1,0:T(8,128)(2,1)} %copy-done.8) | copy-start | bytes 1769476
  293.7 7.0 %copy-start.7 = (bf16[96,3072]{1,0:T(8,128)(2,1)S(1)}, bf16[96,3072]{1,0:T(8,128)(2,1)}, u32[]{:S(2)}) copy-start(bf16[96,3072]{1,0:T(8,128)(2,1)} %copy-done.6) | copy-start | bytes 1769476
  294.5 7.1 %copy-start.5 = (bf16[96,3072]{1,0:T(8,128)(2,1)S(1)}, bf16[96,3072]{1,0:T(8,128)(2,1)}, u32[]{:S(2)}) copy-start(bf16[96,3072]{1,0:T(8,128)(2,1)} %copy-done.4) | copy-start | bytes 1769476
  295.4 7.1 %copy-start.3 = (bf16[96,3072]{1,0:T(8,128)(2,1)S(1)}, bf16[96,3072]{1,0:T(8,128)(2,1)}, u32[]{:S(2)}) copy-start(bf16[96,3072]{1,0:T(8,128)(2,1)} %param.16) | copy-start | bytes 1769476
  298.9 9.2 %copy-start.26 = (bf16[96,3072]{1,0:T(8,128)(2,1)S(1)}, bf16[96,3072]{1,0:T(8,128)(2,1)}, u32[]{:S(2)}) copy-start(bf16[96,3072]{1,0:T(8,128)(2,1)} %copy-done.24) | copy-start | bytes 1769476
  329.0 2.9 copy-start.29
  335.3 6.1 %copy-start.33 = (f32[3,1536]{1,0:T(4,128)S(1)}, f32[3,1536]{1,0:T(4,128)}, u32[]{:S(2)}) copy-start(f32[3,1536]{1,0:T(4,128)} %get-tuple-element.13) | copy-start | bytes 55300
  336.2 4.5 %collective-permute-start.1 = (bf16[3,8,8,768]{3,1,0,2:T(8,128)(2,1)S(1)}, bf16[3,8,8,768]{3,1,0,2:T(8,128)(2,1)S(1)}, u32[]{:S(2)}, u32[]{:S(2)}) collective-permute-start(bf16[3,8,8,768]{3,1,0,2:T(8,128)(2,1)S(1)} %slice.59), channel_id=1, source_target_pairs={{0,15},{1,0},{2,1},{3,2},{4,3},{5,4},{6,5},{7,6},{8,7},{9,8},{10,9... | collective-permute-start | bytes 884744 | tf_op jit(solution)/shard_map/ppermute | solution.py:35
  340.8 4.0 %copy-start.31 = (f32[3,1536]{1,0:T(4,128)S(1)}, f32[3,1536]{1,0:T(4,128)}, u32[]{:S(2)}) copy-start(f32[3,1536]{1,0:T(4,128)} %get-tuple-element.9) | copy-start | bytes 55300
  340.8 4.0 %copy-start.32 = (f32[3,1536]{1,0:T(4,128)S(1)}, f32[3,1536]{1,0:T(4,128)}, u32[]{:S(2)}) copy-start(f32[3,1536]{1,0:T(4,128)} %get-tuple-element.10) | copy-start | bytes 55300
  345.5 24.0 %copy-start.30 = (f32[3,1536]{1,0:T(4,128)S(1)}, f32[3,1536]{1,0:T(4,128)}, u32[]{:S(2)}) copy-start(f32[3,1536]{1,0:T(4,128)} %get-tuple-element.8) | copy-start | bytes 55300
  345.5 27.1 %copy-start.1 = (bf16[32,6,1536]{2,0,1:T(8,128)(2,1)S(1)}, bf16[32,6,1536]{2,0,1:T(8,128)(2,1)}, u32[]{:S(2)}) copy-start(bf16[32,6,1536]{2,0,1:T(8,128)(2,1)} %param.12) | copy-start | bytes 1769476
Sparse Core Ops, SparseCore 0:
  9.6 81.8 all-gather.3
  93.8 46.5 all-gather.5
  179.9 97.0 all-gather.7
